TPU v7x, 32 devices: a whole 2x2x4 slice. The times are simulated.
32 devices in a mesh: cp: 16 (over z, y, core), vocab: 2 (over x).
Axes of the slice: x: 2, y: 2, z: 4, core: 2. Of those that a mesh axis runs over, the one named last changes fastest.
Arguments:
- queries: bfloat16 [2048, 4096], P('cp', 'vocab'), may hold values from -160 to 160
- key_states: bfloat16 [2048, 1024], P('cp', 'vocab'), may hold values from -6 to 6
- value_states: bfloat16 [2048, 1024], P('cp', 'vocab'), may hold values from -6 to 6
- out_grad: bfloat16 [2048, 4096], P('cp', 'vocab'), may hold values from -6 to 6
- o_weight: bfloat16 [4096, 4096], P('vocab'), may hold values from -0.09375 to 0.09375
- span_order: int32 [32], replicated, may hold values from 0 to 31, each once
Outputs:
- query_grad: float32 [2048, 4096], P('cp', 'vocab')
- key_grad: float32 [2048, 1024], P('cp', 'vocab')
- value_grad: float32 [2048, 1024], P('cp', 'vocab')
Inputs may be any that keep to these rules, and one draw needn't show every extreme that they name: `span_order`: each of the 32 span indices once.
All inputs are finite; a program needn't handle non-finite values.
Results may differ from a plain program's by a relative error of at most 0.014.
Values may be sent and summed in bfloat16 or wider, within the bound.
A program may use at most 64 MiB of HBM per device.

v0:
```python
import jax
import jax.numpy as jnp
from jax import lax
from jax.sharding import PartitionSpec as P

HEADS = 32
KV_HEADS = 8
HEAD_DIM = 128


def positions(span_order, span_rows):
    offsets = jnp.arange(span_rows, dtype=jnp.int32)
    return (span_order[:, None] * span_rows + offsets[None, :]).reshape(-1)


def block_scores(query_block, key_block, query_places, key_places, factor):
    scores = (
        jnp.einsum("qkgd,skd->kgqs", query_block, key_block, preferred_element_type=jnp.float32)
        * factor
    )
    visible = key_places[None, :] <= query_places[:, None]
    return jnp.where(visible, scores, -jnp.inf)


def local(queries, key_states, value_states, out_grad, o_weight, span_order):
    own_rows = queries.shape[0]
    kv_width = key_states.shape[1]
    kv_heads = kv_width // HEAD_DIM
    groups = HEADS // KV_HEADS
    factor = HEAD_DIM ** (-0.5)
    upstream = lax.dot_general(
        lax.all_gather(out_grad, "vocab", axis=1, tiled=True),
        o_weight,
        (((1,), (1,)), ((), ())),
        preferred_element_type=jnp.float32,
    ).astype(jnp.bfloat16)
    places = positions(span_order, own_rows // 2)
    seq_len = places.shape[0]
    own_places = lax.dynamic_slice_in_dim(places, lax.axis_index("cp") * own_rows, own_rows, 0)
    query_heads = queries.reshape(own_rows, kv_heads, groups, HEAD_DIM)
    upstream_heads = upstream.reshape(own_rows, kv_heads, groups, HEAD_DIM)
    key_all, value_all = (
        lax.all_gather(key_states, "cp", axis=0, tiled=True),
        lax.all_gather(value_states, "cp", axis=0, tiled=True),
    )
    key_all = key_all.reshape(seq_len, kv_heads, HEAD_DIM)
    value_all = value_all.reshape(seq_len, kv_heads, HEAD_DIM)
    block_rows = own_rows * 8
    block_count = seq_len // block_rows
    block_ids = jnp.arange(block_count, dtype=jnp.int32)
    stat_shape = (kv_heads, groups, own_rows)

    def key_block(block_index):
        offset = block_index * block_rows
        return (
            lax.dynamic_slice_in_dim(key_all, offset, block_rows, 0),
            lax.dynamic_slice_in_dim(value_all, offset, block_rows, 0),
            lax.dynamic_slice_in_dim(places, offset, block_rows, 0),
        )

    def stats_step(carried, block_index):
        running, totals, delta_acc = carried
        keys_now, values_now, places_now = key_block(block_index)
        scores = block_scores(query_heads, keys_now, own_places, places_now, factor)
        newest = jnp.maximum(running, jnp.max(scores, axis=3))
        rescale = jnp.exp(running - newest)
        raised = jnp.exp(scores - newest[..., None])
        grad_probs = jnp.einsum(
            "qkgd,skd->kgqs", upstream_heads, values_now, preferred_element_type=jnp.float32
        )
        totals = totals * rescale + jnp.sum(raised, axis=3)
        delta_acc = delta_acc * rescale + jnp.sum(raised * grad_probs, axis=3)
        return ((newest, totals, delta_acc), None)

    start_stats = (
        jnp.full(stat_shape, -1e30, jnp.float32),
        jnp.zeros(stat_shape, jnp.float32),
        jnp.zeros(stat_shape, jnp.float32),
    )
    (running, totals, delta_acc), unused = lax.scan(stats_step, start_stats, block_ids)
    logsum = running + jnp.log(totals)
    deltas = delta_acc / totals

    def grad_pieces(block_index):
        keys_now, values_now, places_now = key_block(block_index)
        scores = block_scores(query_heads, keys_now, own_places, places_now, factor)
        weights = jnp.exp(scores - logsum[..., None])
        grad_probs = jnp.einsum(
            "qkgd,skd->kgqs", upstream_heads, values_now, preferred_element_type=jnp.float32
        )
        grad_scores = (weights * (grad_probs - deltas[..., None])).astype(jnp.bfloat16)
        return (keys_now, weights, grad_scores)

    query_zeros = jnp.zeros((own_rows, kv_heads, groups, HEAD_DIM), jnp.float32)

    def grad_step(carried, block_index):
        keys_now, weights, grad_scores = grad_pieces(block_index)
        carried = (
            carried
            + jnp.einsum(
                "kgqs,skd->qkgd", grad_scores, keys_now, preferred_element_type=jnp.float32
            )
            * factor
        )
        key_term = (
            jnp.einsum(
                "kgqs,qkgd->skd", grad_scores, query_heads, preferred_element_type=jnp.float32
            )
            * factor
        )
        value_term = jnp.einsum(
            "kgqs,qkgd->skd",
            weights.astype(jnp.bfloat16),
            upstream_heads,
            preferred_element_type=jnp.float32,
        )
        joined = jnp.concatenate(
            (key_term.reshape(block_rows, kv_width), value_term.reshape(block_rows, kv_width)),
            axis=1,
        )
        return (carried, joined)

    query_total, stacked = lax.scan(grad_step, query_zeros, block_ids)
    terms = stacked.reshape(seq_len, 2 * kv_width)
    mine = lax.psum_scatter(
        terms.astype(jnp.bfloat16), "cp", scatter_dimension=0, tiled=True
    ).astype(jnp.float32)
    key_grad = mine[:, :kv_width]
    value_grad = mine[:, kv_width:]
    query_grad = query_total.reshape(own_rows, kv_heads * groups * HEAD_DIM)
    return (query_grad, key_grad, value_grad)


def solution(mesh):
    return jax.shard_map(
        local,
        mesh=mesh,
        in_specs=(
            P("cp", "vocab"),
            P("cp", "vocab"),
            P("cp", "vocab"),
            P("cp", "vocab"),
            P("vocab", None),
            P(),
        ),
        out_specs=(P("cp", "vocab"), P("cp", "vocab"), P("cp", "vocab")),
        check_vma=False,
    )
```

profile of v0, /device:TPU:0, one launch (start us, length us, event | category | flops | bytes accessed | tf_op | source)
XLA Modules:
  0.0 253.9 jit_solution(16052969904517764224)
XLA Ops:
  7.2 0.7 all-gather.8.cloned.1.call-update
  7.9 1.7 copy.27
  9.7 1.7 copy.29
  11.5 0.7 broadcast_multiply_fusion
  12.3 1.3 copy.28
  13.6 1.0 copy.31
  14.7 18.9 %all-gather.8.cloned.1.call-done = bf16[128,4096]{1,0:T(8,128)(2,1)} async-done(((bf16[128,2048]{1,0:T(8,128)(2,1)}), bf16[128,4096]{1,0:T(8,128)(2,1)}) %all-gather.8.cloned.1.call-update) | async-done | bytes 1048592 | tf_op jit(solution)/shard_map/all_gather | solution.py:32
  33.6 11.8 %convolution_convert_fusion = bf16[128,2048]{1,0:T(8,128)(2,1)S(1)} fusion(bf16[128,4096]{1,0:T(8,128)(2,1)} %all-gather.8.cloned.1.call-done, bf16[2048,4096]{1,0:T(8,128)(2,1)} %param.14), kind=kOutput, calls=%fused_computation.51 | convolution fusion | flops 2147745792 | bytes 18350080 | tf_op jit(solution)/shard_map/dot_general | solution.py:31
  45.3 0.4 reshape.49
  45.7 1.0 copy.33
  46.7 1.3 copy.36
  47.9 29.4 %all-gather.4.cloned.1.call-done = bf16[2048,512]{0,1:T(8,128)(2,1)} async-done(((bf16[128,512]{0,1:T(8,128)(2,1)}), bf16[2048,512]{0,1:T(8,128)(2,1)}) %all-gather.4.cloned.1.call-update) | async-done | bytes 2097168 | tf_op jit(solution)/shard_map/all_gather | solution.py:43
  77.4 3.0 %copy.34 = bf16[2048,4,128]{2,0,1:T(8,128)(2,1)S(1)} copy(bf16[2048,4,128]{0,2,1:T(8,128)(2,1)} %bitcast.158) | data formatting | bytes 4194304
  80.4 39.9 %all-gather.6.cloned.1.call-done = bf16[2048,512]{0,1:T(8,128)(2,1)} async-done(((bf16[128,512]{0,1:T(8,128)(2,1)}), bf16[2048,512]{0,1:T(8,128)(2,1)}) %all-gather.6.cloned.1.call-update) | async-done | bytes 2097168 | tf_op jit(solution)/shard_map/all_gather | solution.py:44
  120.2 4.0 %copy.32 = bf16[2048,4,128]{2,0,1:T(8,128)(2,1)} copy(bf16[2048,4,128]{0,2,1:T(8,128)(2,1)} %bitcast.159) | data formatting | bytes 4194304
  124.2 16.3 %while.28 = (s32[]{:T(128)}, f32[4,4,128]{2,1,0:T(4,128)S(1)}, f32[4,4,128]{2,1,0:T(4,128)S(1)}, f32[4,4,128]{2,1,0:T(4,128)S(1)}, s32[2]{0:T(128)S(1)}, /*index...) while((s32[]{:T(128)}, f32[4,4,128]{2,1,0:T(4,128)S(1)}, ...), condition=%wide.region_4.5_spmd.clone, body=%wide.region_0.4_spmd.clone.sunk | while | flops 1099053056 | bytes 39482140 | solution.py:80
  124.2 0.6 dynamic_slice.70
  125.5 0.2 broadcast_compare_fusion.4
  125.7 2.4 fusion.75
  128.2 2.5 fusion.76
  130.6 1.7 fusion.77
  132.4 0.6 dynamic_slice.70
  133.7 0.2 broadcast_compare_fusion.4
  133.9 2.4 fusion.75
  136.4 2.4 fusion.76
  138.8 1.7 fusion.77
  140.6 26.7 %while.29 = (s32[]{:T(128)}, f32[128,4,4,128]{0,3,2,1:T(8,128)S(1)}, bf16[2,1024,1024]{1,2,0:T(8,128)(2,1)}, s32[2]{0:T(128)S(1)}, bf16[2048,4,128]{2,0,1:T(8,12...) while((s32[]{:T(128)}, ...), condition=%wide.region_6.7_spmd.clone, body=%wide.region_5.6_spmd.clone.sunk | while | flops 2711486464 | bytes 97948544 | solution.py:123
  140.6 0.6 dynamic_slice.75
  142.1 2.3 fusion.89
  144.4 2.1 fusion.92
  146.6 2.5 fusion.90
  149.1 1.1 fusion.91
  150.2 1.5 bitcast_multiply_fusion.3
  151.7 0.3 fusion.93
  152.0 1.9 copy-done.3
  153.9 0.6 dynamic_slice.75
  155.2 0.2 broadcast_compare_fusion.5
  155.4 2.3 fusion.89
  157.7 2.1 fusion.92
  159.9 2.5 fusion.90
  162.4 1.1 fusion.91
  163.5 1.5 bitcast_multiply_fusion.3
  165.0 0.3 fusion.93
  165.3 1.9 copy-done.3
  167.3 6.2 %copy.38 = bf16[2,1024,1024]{2,1,0:T(8,128)(2,1)} copy(bf16[2,1024,1024]{1,2,0:T(8,128)(2,1)} %get-tuple-element.129) | data formatting | bytes 8388608 | tf_op jit(solution)/shard_map/convert_element_type | solution.py:126
  173.5 1.3 copy.51
  174.8 70.7 %reduce-scatter.2.cloned.1.call-done = bf16[128,1024]{1,0:T(8,128)(2,1)} async-done(((bf16[2048,1024]{1,0:T(8,128)(2,1)}), bf16[128,1024]{1,0:T(8,128)(2,1)}) %reduce-scatter.2.cloned.1.call-update) | async-done | bytes 262160 | tf_op jit(solution)/shard_map/reduce_scatter | solution.py:125
  245.5 1.8 fusion.38
  (57 shorter events, 0.8 us)
Async XLA Ops:
  7.2 26.4 %all-gather.8.cloned.1.call-start = ((), (), s32[]{:S(2)}) async-start(), calls=%async_computation.3 | async-start | bytes 1572864 | tf_op jit(solution)/shard_map/all_gather | solution.py:32
  7.9 69.5 %all-gather.4.cloned.1.call-start = ((), (), s32[]{:S(2)}) async-start(), calls=%async_computation.1 | async-start | bytes 2228224 | tf_op jit(solution)/shard_map/all_gather | solution.py:43
  9.6 110.6 %all-gather.6.cloned.1.call-start = ((), (), s32[]{:S(2)}) async-start(), calls=%async_computation.2 | async-start | bytes 2228224 | tf_op jit(solution)/shard_map/all_gather | solution.py:44
  11.4 234.1 %reduce-scatter.2.cloned.1.call-start = ((), (), s32[]{:S(2)}) async-start(), calls=%async_computation.4 | async-start | bytes 4456448 | tf_op jit(solution)/shard_map/reduce_scatter | solution.py:125
  13.6 31.7 %copy-start = (bf16[128,2048]{0,1:T(8,128)(2,1)}, bf16[128,2048]{0,1:T(8,128)(2,1)S(1)}, u32[]{:S(2)}) copy-start(bf16[128,2048]{0,1:T(8,128)(2,1)S(1)} %copy.28) | copy-start | bytes 1572868
  125.4 2.7 %copy-start.4 = (bf16[2048,4,128]{2,0,1:T(8,128)(2,1)S(1)}, bf16[2048,4,128]{2,0,1:T(8,128)(2,1)}, u32[]{:S(2)}) copy-start(bf16[2048,4,128]{2,0,1:T(8,128)(2,1)} %get-tuple-element.494) | copy-start | bytes 6291460 | tf_op jit(solution)/shard_map/while
  125.5 2.7 %copy-start.7 = (bf16[128,4,4,128]{3,0,2,1:T(8,128)(2,1)S(1)}, bf16[128,4,4,128]{3,0,2,1:T(8,128)(2,1)}, u32[]{:S(2)}) copy-start(bf16[128,4,4,128]{3,0,2,1:T(8,128)(2,1)} %get-tuple-element.495) | copy-start | bytes 1572868 | tf_op jit(solution)/shard_map/while
  133.6 2.7 %copy-start.4 = (bf16[2048,4,128]{2,0,1:T(8,128)(2,1)S(1)}, bf16[2048,4,128]{2,0,1:T(8,128)(2,1)}, u32[]{:S(2)}) copy-start(bf16[2048,4,128]{2,0,1:T(8,128)(2,1)} %get-tuple-element.494) | copy-start | bytes 6291460 | tf_op jit(solution)/shard_map/while
  133.6 2.7 %copy-start.7 = (bf16[128,4,4,128]{3,0,2,1:T(8,128)(2,1)S(1)}, bf16[128,4,4,128]{3,0,2,1:T(8,128)(2,1)}, u32[]{:S(2)}) copy-start(bf16[128,4,4,128]{3,0,2,1:T(8,128)(2,1)} %get-tuple-element.495) | copy-start | bytes 1572868 | tf_op jit(solution)/shard_map/while
  141.8 2.5 copy-start.6
  144.4 2.2 copy-start.5
  146.5 3.6 %copy-start.1 = (bf16[128,4,4,128]{0,3,2,1:T(8,128)(2,1)S(1)}, bf16[128,4,4,128]{0,3,2,1:T(8,128)(2,1)}, u32[]{:S(2)}) copy-start(bf16[128,4,4,128]{0,3,2,1:T(8,128)(2,1)} %get-tuple-element.539) | copy-start | bytes 1572868 | tf_op jit(solution)/shard_map/while
  149.1 2.6 %copy-start.2 = (bf16[2,1024,1024]{1,2,0:T(8,128)(2,1)S(1)}, bf16[2,1024,1024]{1,2,0:T(8,128)(2,1)}, u32[]{:S(2)}) copy-start(bf16[2,1024,1024]{1,2,0:T(8,128)(2,1)} %get-tuple-element.518) | copy-start | bytes 12582916 | tf_op jit(solution)/shard_map/while
  152.0 1.9 copy-start.3
  155.2 2.5 copy-start.6
  157.7 2.2 copy-start.5
  159.9 3.6 %copy-start.1 = (bf16[128,4,4,128]{0,3,2,1:T(8,128)(2,1)S(1)}, bf16[128,4,4,128]{0,3,2,1:T(8,128)(2,1)}, u32[]{:S(2)}) copy-start(bf16[128,4,4,128]{0,3,2,1:T(8,128)(2,1)} %get-tuple-element.539) | copy-start | bytes 1572868 | tf_op jit(solution)/shard_map/while
  162.4 2.6 %copy-start.2 = (bf16[2,1024,1024]{1,2,0:T(8,128)(2,1)S(1)}, bf16[2,1024,1024]{1,2,0:T(8,128)(2,1)}, u32[]{:S(2)}) copy-start(bf16[2,1024,1024]{1,2,0:T(8,128)(2,1)} %get-tuple-element.518) | copy-start | bytes 12582916 | tf_op jit(solution)/shard_map/while
  165.3 1.9 copy-start.3
Sparse Core Ops, SparseCore 0:
  9.5 23.9 all-gather.7
  36.3 41.0 all-gather.3
  80.1 40.1 all-gather.5
  173.6 71.8 reduce-scatter.1
where the time goes:
time: 254 us
  waiting for transfers between devices  160 us (63%)
  matrix products  40.6 us (16%)
  local copies, waits for them, and re-layouts  31.1 us (12%)
  between operations  13.9 us (5%)
  other arithmetic  5.53 us (2%)
  loops' own time  3.08 us (1%)
    reduce_scatter x1, waiting for transfers between devices, local(): lax.psum_scatter(terms.astype(jnp.bfloat16), 'cp', scatter_dimension=0, t...  70.7 us
    all_gather x1, waiting for transfers between devices, local(): lax.all_gather(value_states, 'cp', axis=0, tiled=True)  39.9 us
    all_gather x1, waiting for transfers between devices, local(): lax.all_gather(key_states, 'cp', axis=0, tiled=True)  29.4 us
    all_gather x1, waiting for transfers between devices, local(): lax.all_gather(out_grad, 'vocab', axis=1, tiled=True)  18.9 us
    unnamed x10, local copies, waits for them, and re-layouts  14.9 us
    dot_general x1, matrix products, local(): lax.dot_general(lax.all_gather(out_grad, 'vocab', axis=1, tiled=True), o_...  11.8 us
    dot_general x4, matrix products, block_scores(): jnp.einsum('qkgd,skd->kgqs', query_block, key_block, preferred_element_ty...  9.46 us
    convert_element_type x1, local copies, waits for them, and re-layouts, local(): terms.astype(jnp.bfloat16)  6.24 us
  transfers between devices with their start and end apart: 4, of which 4 were waited for; matrix products, arithmetic and copies ran while one was open for 10% of the time, Pallas kernels for 0%

commit v1 on v0

--- a/solution.py
+++ b/solution.py
@@ -40,7 +40,10 @@
     query_heads = queries.reshape(own_rows, kv_heads, groups, HEAD_DIM)
     upstream_heads = upstream.reshape(own_rows, kv_heads, groups, HEAD_DIM)
     key_all, value_all = (
-        lax.all_gather(key_states, "cp", axis=0, tiled=True),
+        jnp.concatenate(
+            lax.all_to_all(jnp.stack([key_states for _ in range(lax.axis_size("cp"))]), "cp", 0, 0),
+            axis=0,
+        ),
         lax.all_gather(value_states, "cp", axis=0, tiled=True),
     )
     key_all = key_all.reshape(seq_len, kv_heads, HEAD_DIM)

time: 254 us -> 230 us (0.906)
  waiting for transfers between devices: 160 us -> 121 us
  starting transfers between devices: 0.16 us -> 7.58 us
  local copies, waits for them, and re-layouts: 31.1 us -> 37.4 us
    all_gather x1 -> x0, waiting for transfers between devices: 29.4 us -> none  [local(): lax.all_gather(key_states, 'cp', axis=0, tiled=True)]
    all_gather x1, waiting for transfers between devices: 18.9 us -> 10.3 us  [local(): lax.all_gather(out_grad, 'vocab', axis=1, tiled=True)]
    all_to_all x0 -> x1, starting transfers between devices: none -> 7.46 us  [local(): lax.all_to_all(jnp.stack([key_states for _ in range(lax.axis_size('cp'))]...]
    another operation x0 -> x2, local copies, waits for them, and re-layouts: none -> 4.08 us  [the longest x1 2.33 us: local(): key_all = key_all.reshape(seq_len, kv_heads, HEAD_DIM)]
    all_to_all x0 -> x1, local copies, waits for them, and re-layouts: none -> 2.94 us  [local(): lax.all_to_all(jnp.stack([key_states for _ in range(lax.axis_size('cp'))]...]
  transfers between devices with their start and end apart: 4 -> 4, of which waited for: 4 -> 3; matrix products, arithmetic and copies ran while one was open for 10% -> 12% of each run, Pallas kernels for 0% -> 0%
where the time goes in v1:
time: 230 us; the launch traced here: 229 us
  waiting for transfers between devices  121 us (53%)
  matrix products  40.6 us (18%)
  local copies, waits for them, and re-layouts  37.4 us (16%)
  between operations  13.9 us (6%)
  starting transfers between devices  7.58 us (3%)
  other arithmetic  5.54 us (2%)
  loops' own time  3.28 us (1%)
    reduce_scatter x1, waiting for transfers between devices, local(): lax.psum_scatter(terms.astype(jnp.bfloat16), 'cp', scatter_dimension=0, t...  70.6 us
    all_gather x1, waiting for transfers between devices, local(): lax.all_gather(value_states, 'cp', axis=0, tiled=True)  39.2 us
    unnamed x10, local copies, waits for them, and re-layouts  14.2 us
    dot_general x1, matrix products, local(): lax.dot_general(lax.all_gather(out_grad, 'vocab', axis=1, tiled=True), o_...  11.8 us
    all_gather x1, waiting for transfers between devices, local(): lax.all_gather(out_grad, 'vocab', axis=1, tiled=True)  10.3 us
    dot_general x4, matrix products, block_scores(): jnp.einsum('qkgd,skd->kgqs', query_block, key_block, preferred_element_ty...  9.46 us
    all_to_all x1, starting transfers between devices, local(): lax.all_to_all(jnp.stack([key_states for _ in range(lax.axis_size('cp'))]...  7.46 us
    convert_element_type x1, local copies, waits for them, and re-layouts, local(): terms.astype(jnp.bfloat16)  6.23 us
  transfers between devices with their start and end apart: 4, of which 3 were waited for; matrix products, arithmetic and copies ran while one was open for 12% of the time, Pallas kernels for 0%

profile of v1, /device:TPU:0, one launch (start us, length us, event | category | flops | bytes accessed | tf_op | source)
XLA Modules:
  0.0 229.1 jit_solution(10056433214175790594)
XLA Ops:
  7.2 0.7 all-gather.5.cloned.1.call-update
  7.9 1.7 copy.48
  9.6 1.0 copy.45
  10.7 1.7 stack.2
  12.4 7.5 %all-to-all-start = ((bf16[16,128,512]{1,2,0:T(8,128)(2,1)}), bf16[16,128,512]{1,2,0:T(8,128)(2,1)}, u32[]{:S(2)}, u32[]{:S(2)}) async-start(bf16[16,128,512]{1,2,0:T(8,128)(2,1)} %stack.2), calls=%async_computation | async-start | bytes 4194304 | tf_op jit(solution)/shard_map/all_to_all | solution.py:44
  20.0 0.7 broadcast_multiply_fusion
  20.8 1.3 copy.47
  22.1 1.0 copy.50
  23.2 10.3 %all-gather.5.cloned.1.call-done = bf16[128,4096]{1,0:T(8,128)(2,1)} async-done(((bf16[128,2048]{1,0:T(8,128)(2,1)}), bf16[128,4096]{1,0:T(8,128)(2,1)}) %all-gather.5.cloned.1.call-update) | async-done | bytes 1048592 | tf_op jit(solution)/shard_map/all_gather | solution.py:32
  33.6 11.8 %convolution_convert_fusion = bf16[128,2048]{1,0:T(8,128)(2,1)S(1)} fusion(bf16[128,4096]{1,0:T(8,128)(2,1)} %all-gather.5.cloned.1.call-done, bf16[2048,4096]{1,0:T(8,128)(2,1)} %param.14), kind=kOutput, calls=%fused_computation.51 | convolution fusion | flops 2147745792 | bytes 18350080 | tf_op jit(solution)/shard_map/dot_general | solution.py:31
  45.3 0.4 reshape.47
  45.7 1.0 copy.52
  46.6 1.3 copy.55
  47.9 39.2 %all-gather.3.cloned.1.call-done = bf16[2048,512]{0,1:T(8,128)(2,1)} async-done(((bf16[128,512]{0,1:T(8,128)(2,1)}), bf16[2048,512]{0,1:T(8,128)(2,1)}) %all-gather.3.cloned.1.call-update) | async-done | bytes 2097168 | tf_op jit(solution)/shard_map/all_gather | solution.py:47
  87.1 3.9 %copy.51 = bf16[2048,4,128]{2,0,1:T(8,128)(2,1)} copy(bf16[2048,4,128]{0,2,1:T(8,128)(2,1)} %bitcast.159) | data formatting | bytes 4194304
  91.0 2.9 %copy.46 = bf16[16,128,512]{1,0,2:T(8,128)(2,1)S(1)} copy(bf16[16,128,512]{1,2,0:T(8,128)(2,1)} %all-to-all-done) | data formatting | bytes 4194304 | tf_op jit(solution)/shard_map/all_to_all | solution.py:44
  94.0 2.3 %reshape_reshape.3 = bf16[2048,4,128]{0,2,1:T(8,128)(2,1)} reshape(bf16[16,128,512]{1,0,2:T(8,128)(2,1)S(1)} %copy.46) | data formatting | bytes 4194304 | tf_op jit(solution)/shard_map/reshape;reshape | solution.py:49
  96.3 3.0 %copy.53 = bf16[2048,4,128]{2,0,1:T(8,128)(2,1)S(1)} copy(bf16[2048,4,128]{0,2,1:T(8,128)(2,1)} %reshape_reshape.3) | data formatting | bytes 4194304
  99.4 16.4 %while.28 = (s32[]{:T(128)}, f32[4,4,128]{2,1,0:T(4,128)S(1)}, f32[4,4,128]{2,1,0:T(4,128)S(1)}, f32[4,4,128]{2,1,0:T(4,128)S(1)}, s32[2]{0:T(128)S(1)}, /*index...) while((s32[]{:T(128)}, f32[4,4,128]{2,1,0:T(4,128)S(1)}, ...), condition=%wide.region_4.5_spmd.clone, body=%wide.region_0.4_spmd.clone.sunk | while | flops 1099053056 | bytes 39482140 | solution.py:83
  99.4 0.6 dynamic_slice.70
  100.9 2.4 %fusion.75 = (f32[4,4,128]{2,1,0:T(4,128)S(1)}, f32[4,1024,128,4]{2,1,3,0:T(8,128)S(1)}) fusion(pred[128,1024]{0,1:T(8,128)(4,1)S(1)} %broadcast_compare_fusion.4, bf16[128,4,4,128]{3,0,2,1:T(8,128)(2,1)} %get-tuple-element.516, bf16[2048,4,128]{2,0,1:T(8,128)(2,1)S(1)} %get-tuple-element.515, s32[]{:T(128)S(6)} %select_n.52), kind=kOutput, calls=%fused_computation.5.clone.1 | convolution fusion | flops 543160320 | bytes 10100740 | tf_op jit(solution)/shard_map/while/body/eval_jaxpr/qkgd,skd->kgqs/dot_general | solution.py:18
  103.3 2.5 %fusion.76 = f32[4,4,128]{2,1,0:T(4,128)S(1)} fusion(f32[4,1024,128,4]{2,1,3,0:T(8,128)S(1)} %get-tuple-element.463, f32[4,4,128]{2,1,0:T(4,128)S(1)} %select_maximum_fusion.2, pred[128,1024]{0,1:T(8,128)(4,1)S(1)} %broadcast_compare_fusion.4, bf16[128,4,4,128]{3,0,2,1:T(8,128)(2,1)S(1)} %copy-done.7, bf16[2048,4,128]{2,0,1:T(8,128)(2,1)S(1)} %copy-done.4, ...), kind=kOutput, calls=%fused_computation.1.clone.1 | convolution fusion | flops 547354624 | bytes 10108932 | tf_op jit(solution)/shard_map/while/body/eval_jaxpr/qkgd,skd->kgqs/dot_general | solution.py:71
  105.8 1.7 fusion.77
  107.6 0.6 dynamic_slice.70
  109.0 2.4 %fusion.75 = (f32[4,4,128]{2,1,0:T(4,128)S(1)}, f32[4,1024,128,4]{2,1,3,0:T(8,128)S(1)}) fusion(pred[128,1024]{0,1:T(8,128)(4,1)S(1)} %broadcast_compare_fusion.4, bf16[128,4,4,128]{3,0,2,1:T(8,128)(2,1)} %get-tuple-element.516, bf16[2048,4,128]{2,0,1:T(8,128)(2,1)S(1)} %get-tuple-element.515, s32[]{:T(128)S(6)} %select_n.52), kind=kOutput, calls=%fused_computation.5.clone.1 | convolution fusion | flops 543160320 | bytes 10100740 | tf_op jit(solution)/shard_map/while/body/eval_jaxpr/qkgd,skd->kgqs/dot_general | solution.py:18
  111.5 2.5 %fusion.76 = f32[4,4,128]{2,1,0:T(4,128)S(1)} fusion(f32[4,1024,128,4]{2,1,3,0:T(8,128)S(1)} %get-tuple-element.463, f32[4,4,128]{2,1,0:T(4,128)S(1)} %select_maximum_fusion.2, pred[128,1024]{0,1:T(8,128)(4,1)S(1)} %broadcast_compare_fusion.4, bf16[128,4,4,128]{3,0,2,1:T(8,128)(2,1)S(1)} %copy-done.7, bf16[2048,4,128]{2,0,1:T(8,128)(2,1)S(1)} %copy-done.4, ...), kind=kOutput, calls=%fused_computation.1.clone.1 | convolution fusion | flops 547354624 | bytes 10108932 | tf_op jit(solution)/shard_map/while/body/eval_jaxpr/qkgd,skd->kgqs/dot_general | solution.py:71
  114.0 1.7 fusion.77
  115.8 26.9 %while.29 = (s32[]{:T(128)}, f32[128,4,4,128]{0,3,2,1:T(8,128)S(1)}, bf16[2,1024,1024]{1,2,0:T(8,128)(2,1)}, s32[2]{0:T(128)S(1)}, bf16[2048,4,128]{2,0,1:T(8,12...) while((s32[]{:T(128)}, ...), condition=%wide.region_6.7_spmd.clone, body=%wide.region_5.6_spmd.clone.sunk | while | flops 2711486464 | bytes 97948544 | solution.py:126
  116.0 0.6 dynamic_slice.75
  117.4 2.3 fusion.89
  119.7 2.1 fusion.92
  121.9 2.5 %fusion.90 = bf16[4,4,128,1024]{2,3,1,0:T(8,128)(2,1)S(1)} fusion(f32[4,1024,128,4]{2,1,3,0:T(8,128)S(1)} %fusion.89, f32[4,4,128]{2,1,0:T(4,128)S(1)} %get-tuple-element.566, f32[4,4,128]{2,1,0:T(4,128)S(1)} %get-tuple-element.563, pred[128,1024]{0,1:T(8,128)(4,1)S(1)} %broadcast_compare_fusion.5, bf16[128,4,4,128]{0,3,2,1:T(8,128)(2,1)S(1)} %copy-done.6, ...), kind=kOutput, calls=%fused_computation.22.clone.1 | convolution fusion | flops 549453824 | bytes 14303236 | tf_op jit(solution)/shard_map/while/body/eval_jaxpr/qkgd,skd->kgqs/dot_general | solution.py:91
  124.5 1.1 fusion.91
  125.6 1.5 bitcast_multiply_fusion.3
  127.1 0.3 fusion.93
  127.4 1.9 copy-done.3
  129.3 0.6 dynamic_slice.75
  130.8 2.3 fusion.89
  133.1 2.1 fusion.92
  135.3 2.5 %fusion.90 = bf16[4,4,128,1024]{2,3,1,0:T(8,128)(2,1)S(1)} fusion(f32[4,1024,128,4]{2,1,3,0:T(8,128)S(1)} %fusion.89, f32[4,4,128]{2,1,0:T(4,128)S(1)} %get-tuple-element.566, f32[4,4,128]{2,1,0:T(4,128)S(1)} %get-tuple-element.563, pred[128,1024]{0,1:T(8,128)(4,1)S(1)} %broadcast_compare_fusion.5, bf16[128,4,4,128]{0,3,2,1:T(8,128)(2,1)S(1)} %copy-done.6, ...), kind=kOutput, calls=%fused_computation.22.clone.1 | convolution fusion | flops 549453824 | bytes 14303236 | tf_op jit(solution)/shard_map/while/body/eval_jaxpr/qkgd,skd->kgqs/dot_general | solution.py:91
  137.8 1.1 fusion.91
  138.9 1.5 bitcast_multiply_fusion.3
  140.4 0.3 fusion.93
  140.7 1.9 copy-done.3
  142.6 6.2 %copy.57 = bf16[2,1024,1024]{2,1,0:T(8,128)(2,1)} copy(bf16[2,1024,1024]{1,2,0:T(8,128)(2,1)} %get-tuple-element.129) | data formatting | bytes 8388608 | tf_op jit(solution)/shard_map/convert_element_type | solution.py:129
  148.9 1.3 copy.70
  150.2 70.6 %reduce-scatter.2.cloned.1.call-done = bf16[128,1024]{1,0:T(8,128)(2,1)} async-done(((bf16[2048,1024]{1,0:T(8,128)(2,1)}), bf16[128,1024]{1,0:T(8,128)(2,1)}) %reduce-scatter.2.cloned.1.call-update) | async-done | bytes 262160 | tf_op jit(solution)/shard_map/reduce_scatter | solution.py:128
  220.8 1.8 fusion.38
  (59 shorter events, 1.4 us)
Async XLA Ops:
  7.2 26.4 %all-gather.5.cloned.1.call-start = ((), (), s32[]{:S(2)}) async-start(), calls=%async_computation.3 | async-start | bytes 1572864 | tf_op jit(solution)/shard_map/all_gather | solution.py:32
  7.9 79.2 %all-gather.3.cloned.1.call-start = ((), (), s32[]{:S(2)}) async-start(), calls=%async_computation.2 | async-start | bytes 2228224 | tf_op jit(solution)/shard_map/all_gather | solution.py:47
  12.4 78.6 %all-to-all-start = ((bf16[16,128,512]{1,2,0:T(8,128)(2,1)}), bf16[16,128,512]{1,2,0:T(8,128)(2,1)}, u32[]{:S(2)}, u32[]{:S(2)}) async-start(bf16[16,128,512]{1,2,0:T(8,128)(2,1)} %stack.2), calls=%async_computation | async-start | bytes 4194304 | tf_op jit(solution)/shard_map/all_to_all | solution.py:44
  19.9 200.9 %reduce-scatter.2.cloned.1.call-start = ((), (), s32[]{:S(2)}) async-start(), calls=%async_computation.4 | async-start | bytes 4456448 | tf_op jit(solution)/shard_map/reduce_scatter | solution.py:128
  22.1 23.2 %copy-start = (bf16[128,2048]{0,1:T(8,128)(2,1)}, bf16[128,2048]{0,1:T(8,128)(2,1)S(1)}, u32[]{:S(2)}) copy-start(bf16[128,2048]{0,1:T(8,128)(2,1)S(1)} %copy.47) | copy-start | bytes 1572868
  100.6 2.7 %copy-start.4 = (bf16[2048,4,128]{2,0,1:T(8,128)(2,1)S(1)}, bf16[2048,4,128]{2,0,1:T(8,128)(2,1)}, u32[]{:S(2)}) copy-start(bf16[2048,4,128]{2,0,1:T(8,128)(2,1)} %get-tuple-element.517) | copy-start | bytes 6291460 | tf_op jit(solution)/shard_map/while
  100.6 2.7 %copy-start.7 = (bf16[128,4,4,128]{3,0,2,1:T(8,128)(2,1)S(1)}, bf16[128,4,4,128]{3,0,2,1:T(8,128)(2,1)}, u32[]{:S(2)}) copy-start(bf16[128,4,4,128]{3,0,2,1:T(8,128)(2,1)} %get-tuple-element.518) | copy-start | bytes 1572868 | tf_op jit(solution)/shard_map/while
  108.8 2.7 %copy-start.4 = (bf16[2048,4,128]{2,0,1:T(8,128)(2,1)S(1)}, bf16[2048,4,128]{2,0,1:T(8,128)(2,1)}, u32[]{:S(2)}) copy-start(bf16[2048,4,128]{2,0,1:T(8,128)(2,1)} %get-tuple-element.517) | copy-start | bytes 6291460 | tf_op jit(solution)/shard_map/while
  108.8 2.7 %copy-start.7 = (bf16[128,4,4,128]{3,0,2,1:T(8,128)(2,1)S(1)}, bf16[128,4,4,128]{3,0,2,1:T(8,128)(2,1)}, u32[]{:S(2)}) copy-start(bf16[128,4,4,128]{3,0,2,1:T(8,128)(2,1)} %get-tuple-element.518) | copy-start | bytes 1572868 | tf_op jit(solution)/shard_map/while
  117.2 2.5 %copy-start.6 = (bf16[128,4,4,128]{0,3,2,1:T(8,128)(2,1)S(1)}, bf16[128,4,4,128]{0,3,2,1:T(8,128)(2,1)}, u32[]{:S(2)}) copy-start(bf16[128,4,4,128]{0,3,2,1:T(8,128)(2,1)} %get-tuple-element.565) | copy-start | bytes 1572868 | tf_op jit(solution)/shard_map/while
  119.7 2.2 copy-start.5
  121.9 3.6 %copy-start.1 = (bf16[128,4,4,128]{0,3,2,1:T(8,128)(2,1)S(1)}, bf16[128,4,4,128]{0,3,2,1:T(8,128)(2,1)}, u32[]{:S(2)}) copy-start(bf16[128,4,4,128]{0,3,2,1:T(8,128)(2,1)} %get-tuple-element.562) | copy-start | bytes 1572868 | tf_op jit(solution)/shard_map/while
  124.5 2.6 %copy-start.2 = (bf16[2,1024,1024]{1,2,0:T(8,128)(2,1)S(1)}, bf16[2,1024,1024]{1,2,0:T(8,128)(2,1)}, u32[]{:S(2)}) copy-start(bf16[2,1024,1024]{1,2,0:T(8,128)(2,1)} %get-tuple-element.541) | copy-start | bytes 12582916 | tf_op jit(solution)/shard_map/while
  127.3 1.9 copy-start.3
  130.5 2.5 %copy-start.6 = (bf16[128,4,4,128]{0,3,2,1:T(8,128)(2,1)S(1)}, bf16[128,4,4,128]{0,3,2,1:T(8,128)(2,1)}, u32[]{:S(2)}) copy-start(bf16[128,4,4,128]{0,3,2,1:T(8,128)(2,1)} %get-tuple-element.565) | copy-start | bytes 1572868 | tf_op jit(solution)/shard_map/while
  133.1 2.2 copy-start.5
  135.2 3.6 %copy-start.1 = (bf16[128,4,4,128]{0,3,2,1:T(8,128)(2,1)S(1)}, bf16[128,4,4,128]{0,3,2,1:T(8,128)(2,1)}, u32[]{:S(2)}) copy-start(bf16[128,4,4,128]{0,3,2,1:T(8,128)(2,1)} %get-tuple-element.562) | copy-start | bytes 1572868 | tf_op jit(solution)/shard_map/while
  137.8 2.6 %copy-start.2 = (bf16[2,1024,1024]{1,2,0:T(8,128)(2,1)S(1)}, bf16[2,1024,1024]{1,2,0:T(8,128)(2,1)}, u32[]{:S(2)}) copy-start(bf16[2,1024,1024]{1,2,0:T(8,128)(2,1)} %get-tuple-element.541) | copy-start | bytes 12582916 | tf_op jit(solution)/shard_map/while
  140.7 1.9 copy-start.3
Sparse Core Ops, SparseCore 0:
  9.5 23.9 all-gather.4
  36.3 50.7 all-gather.2
  149.0 71.7 reduce-scatter.1
